TPU v7x, 32 devices: a whole 2x2x4 slice. The times are simulated.
32 devices in a mesh: ba: 4 (over x, core), gx: 2 (over y), gy: 4 (over z).
Axes of the slice: x: 2, y: 2, z: 4, core: 2. Of those that a mesh axis runs over, the one named last changes fastest.
Arguments:
- pixels: bfloat16 [112, 224, 6], P(('ba', 'gx'), 'gy'), parts along dimension 0, may hold values from -6 to 6
- conv_weight: bfloat16 [54, 704], replicated, may hold values from -0.875 to 0.875
- input_gain: float32 [704], replicated, may hold values from 0.5 to 1.5
- key_weight: bfloat16 [704, 1024], replicated, may hold values from -0.21875 to 0.21875
- value_weight: bfloat16 [704, 1024], replicated, may hold values from -0.21875 to 0.21875
- latents: bfloat16 [512, 1024], replicated, may hold values from -6 to 6
- latent_gain: float32 [1024], replicated, may hold values from 0.5 to 1.5
- query_weight: bfloat16 [1024, 1024], replicated, as said below
- out_weight: bfloat16 [1024, 1024], replicated, may hold values from -0.1875 to 0.1875
Outputs:
- new_latents: bfloat16 [2048, 1024], P(('ba', 'gx', 'gy')), parts along dimension 0
There are 4 independent parts, one for each index of `ba`. A program takes and returns all parts, laid end to end along the dimension named above; an argument that names none is the same for every part. Nothing has to cross between parts.
Inputs may be any that keep to these rules, and one draw needn't show every extreme that they name: `query_weight`: independent entries, mean zero, of order 3 * 1024 ** -0.5, and up to 20 times that in the columns of some heads.
All inputs are finite; a program needn't handle non-finite values.
Results may differ from a plain program's by a relative error of at most 0.025.
Values may be sent and summed in bfloat16 or wider, within the bound.
A program may use at most 64 MiB of HBM per device.

v0:
```python
import jax
import jax.numpy as jnp
from jax import lax
from jax.sharding import PartitionSpec as P

HEADS = 8
DH = 128


def extended(cells, sides, width):
    for axis, dim in sides:
        count = lax.axis_size(axis)
        ends = count - 1
        head = lax.slice_in_dim(cells, 0, width, axis=dim)
        tail = lax.slice_in_dim(cells, cells.shape[dim] - width, cells.shape[dim], axis=dim)
        cells = jnp.concatenate(
            [
                lax.ppermute(tail, axis, [(i, (i + 1) % count) for i in range(ends)]),
                cells,
                lax.ppermute(head, axis, [((i + 1) % count, i) for i in range(ends)]),
            ],
            axis=dim,
        )
    return cells


def layer_norm(values, gain):
    mean = jnp.mean(values, axis=-1, keepdims=True)
    centred = values - mean
    variance = jnp.mean(centred * centred, axis=-1, keepdims=True)
    return centred * lax.rsqrt(variance + 1e-05) * gain


def project_latents(rows, latent_gain, query_weight):
    lat_normed = layer_norm(rows.astype(jnp.float32), latent_gain).astype(jnp.bfloat16)
    return jnp.dot(lat_normed, query_weight, preferred_element_type=jnp.float32).astype(
        jnp.bfloat16
    )


def on_device(
    pixels,
    conv_weight,
    input_gain,
    key_weight,
    value_weight,
    latents,
    latent_gain,
    query_weight,
    out_weight,
):
    tile_rows, tile_cols = (pixels.shape[0], pixels.shape[1])
    padded = extended(pixels, (("gx", 0), ("gy", 1)), 1)
    patches = jnp.concatenate(
        [
            padded[row_off : row_off + tile_rows, col_off : col_off + tile_cols, :]
            for row_off in range(3)
            for col_off in range(3)
        ],
        axis=-1,
    )
    patches = patches.reshape(tile_rows * tile_cols, -1)
    features = jnp.dot(patches, conv_weight, preferred_element_type=jnp.float32).astype(
        jnp.bfloat16
    )
    normed = layer_norm(features.astype(jnp.float32), input_gain).astype(jnp.bfloat16)
    key_rows = jnp.dot(normed, key_weight, preferred_element_type=jnp.float32).astype(jnp.bfloat16)
    value_rows = jnp.dot(normed, value_weight, preferred_element_type=jnp.float32).astype(
        jnp.bfloat16
    )
    devices = lax.axis_size(("gx", "gy"))
    share = latents.shape[0] // devices
    first_row = lax.axis_index(("gx", "gy")) * share
    queries = project_latents(latents, latent_gain, query_weight)
    scale = 1.0 / DH**0.5

    def one_head(head):
        start = head * DH
        query_head = lax.dynamic_slice_in_dim(queries, start, DH, 1)
        key_head = lax.dynamic_slice_in_dim(key_rows, start, DH, 1)
        value_head = lax.dynamic_slice_in_dim(value_rows, start, DH, 1)
        scores = jnp.dot(query_head, key_head.T, preferred_element_type=jnp.float32) * scale
        top = jnp.max(scores, axis=-1)
        expo = jnp.exp(scores - top[:, None])
        total = jnp.sum(expo, axis=-1)
        summed = jnp.dot(expo.astype(jnp.bfloat16), value_head, preferred_element_type=jnp.float32)
        return (top, total, summed)

    local_top, local_total, local_summed = lax.map(one_head, jnp.arange(HEADS, dtype=jnp.int32))
    global_top = lax.pmax(local_top, ("gx", "gy"))
    factor = jnp.exp(local_top - global_top)
    summed, total = (
        lax.psum_scatter(
            local_summed * factor[..., None], ("gx", "gy"), scatter_dimension=1, tiled=True
        ),
        lax.psum_scatter(local_total * factor, ("gx", "gy"), scatter_dimension=1, tiled=True),
    )
    attended = summed / total[..., None]
    attended = jnp.transpose(attended, (1, 0, 2)).reshape(share, -1).astype(jnp.bfloat16)
    own_rows = lax.dynamic_slice_in_dim(latents, first_row, share, 0)
    result = own_rows.astype(jnp.float32) + jnp.dot(
        attended, out_weight, preferred_element_type=jnp.float32
    )
    return result.astype(jnp.bfloat16)


def solution(mesh):
    return jax.shard_map(
        on_device,
        mesh=mesh,
        in_specs=(P(("ba", "gx"), "gy", None), P(), P(), P(), P(), P(), P(), P(), P()),
        out_specs=P(("ba", "gx", "gy"), None),
        check_vma=False,
    )
```

profile of v0, /device:TPU:0, one launch (start us, length us, event | category | flops | bytes accessed | tf_op | source)
XLA Modules:
  0.0 255.8 jit_solution(18430653766976069483)
XLA Ops:
  6.5 0.9 fusion.37
  7.4 5.0 %collective-permute-start = (bf16[1,56,6]{1,0,2:T(2,128)(2,1)S(1)}, bf16[1,56,6]{1,0,2:T(2,128)(2,1)S(1)}, u32[]{:S(2)}, u32[]{:S(2)}) collective-permute-start(bf16[1,56,6]{1,0,2:T(2,128)(2,1)S(1)} %get-tuple-element.76), channel_id=1, source_target_pairs={{0,4},{1,5},{2,6},{3,7},{8,12},{9,13},{10,14},{11,15},{16,20},{17,... | collective-permute-start | bytes 2024 | tf_op jit(solution)/shard_map/ppermute | solution.py:18
  12.5 1.3 collective-permute-start.1
  13.8 1.4 convert_reduce_fusion.1
  15.2 1.6 fusion.20
  16.9 2.3 convolution_convert_fusion.3
  19.4 3.5 %collective-permute-start.2 = (bf16[16,1,6]{1,0,2:T(8,128)(2,1)S(1)}, bf16[16,1,6]{1,0,2:T(8,128)(2,1)S(1)}, u32[]{:S(2)}, u32[]{:S(2)}) collective-permute-start(bf16[16,1,6]{1,0,2:T(8,128)(2,1)S(1)} %get-tuple-element.75), channel_id=1, source_target_pairs={{0,1},{1,2},{2,3},{4,5},{5,6},{6,7},{8,9},{9,10},{10,11},{12,13},{... | collective-permute-start | bytes 584 | tf_op jit(solution)/shard_map/ppermute | solution.py:18
  22.8 1.3 collective-permute-start.3
  24.3 4.2 %collective-permute-done.3 = bf16[16,1,6]{1,0,2:T(8,128)(2,1)S(1)} collective-permute-done((bf16[16,1,6]{1,0,2:T(8,128)(2,1)S(1)}, bf16[16,1,6]{1,0,2:T(8,128)(2,1)S(1)}, u32[]{:S(2)}, u32[]{:S(2)}) %collective-permute-start.3) | collective-permute-done | bytes 224 | tf_op jit(solution)/shard_map/ppermute | solution.py:20
  29.3 0.6 convert_reduce_fusion
  30.0 0.6 fusion.17
  30.7 2.7 %convolution_convert_fusion = bf16[784,1024]{1,0:T(8,128)(2,1)} fusion(bf16[704,1024]{1,0:T(8,128)(2,1)S(1)} %copy-done.6, bf16[784,704]{1,0:T(8,128)(2,1)S(1)} %get-tuple-element.79, f32[704]{0:T(1024)S(1)} %copy-done.9, f32[784]{0:T(1024)S(1)} %add_rsqrt_fusion, f32[784]{0:T(1024)S(1)} %broadcast_multiply_fusion.1), kind=kOutput, calls=%fused_computation.29 | convolution fusion | flops 1133927424 | bytes 4160384 | tf_op jit(solution)/shard_map/dot_general | solution.py:68
  33.4 2.7 %convolution_convert_fusion.1 = bf16[784,1024]{1,0:T(8,128)(2,1)} fusion(bf16[704,1024]{1,0:T(8,128)(2,1)S(1)} %copy-done.7, bf16[784,704]{1,0:T(8,128)(2,1)S(1)} %get-tuple-element.79, f32[704]{0:T(1024)S(1)} %copy-done.9, f32[784]{0:T(1024)S(1)} %add_rsqrt_fusion, f32[784]{0:T(1024)S(1)} %broadcast_multiply_fusion.1), kind=kOutput, calls=%fused_computation.30 | convolution fusion | flops 1133927424 | bytes 4160384 | tf_op jit(solution)/shard_map/dot_general | solution.py:67
  36.1 41.5 %while.14 = (s32[]{:T(128)}, f32[8,512]{1,0:T(8,128)S(1)}, f32[8,512]{1,0:T(8,128)S(1)}, f32[8,512,128]{2,1,0:T(8,128)}, s32[8]{0:T(128)S(1)}, /*index=5*/bf16[5...) while((s32[]{:T(128)}, f32[8,512]{1,0:T(8,128)S(1)}, ...), condition=%wide.region_7.8_spmd, body=%wide.region_4.7_spmd.sunk | while | flops 208731136 | bytes 5629627 | solution.py:89
  36.1 0.6 dynamic_slice.35
  37.3 1.4 multiply_reduce_fusion.2
  38.7 2.1 fusion.53
  40.8 0.3 fusion.52
  41.2 0.6 dynamic_slice.35
  42.5 1.4 multiply_reduce_fusion.2
  43.9 2.1 fusion.53
  46.0 0.3 fusion.52
  46.4 0.6 dynamic_slice.35
  47.7 1.4 multiply_reduce_fusion.2
  49.1 2.1 fusion.53
  51.6 0.6 dynamic_slice.35
  52.8 1.4 multiply_reduce_fusion.2
  54.2 2.1 fusion.53
  56.8 0.6 dynamic_slice.35
  58.0 1.4 multiply_reduce_fusion.2
  59.4 2.1 fusion.53
  62.0 0.6 dynamic_slice.35
  63.2 1.4 multiply_reduce_fusion.2
  64.6 2.1 fusion.53
  66.7 0.3 fusion.52
  67.2 0.6 dynamic_slice.35
  68.4 1.4 multiply_reduce_fusion.2
  69.8 2.1 fusion.53
  72.4 0.6 dynamic_slice.35
  73.6 1.4 multiply_reduce_fusion.2
  75.0 2.1 fusion.53
  77.6 36.8 %pmax.7 = f32[8,512]{1,0:T(8,128)S(1)} all-reduce(f32[8,512]{1,0:T(8,128)S(1)} %get-tuple-element.50), channel_id=1, replica_groups=mesh['ba'=4,'gx'=2,'gy'=4] {'gx','gy'}, use_global_device_ids=true, to_apply=%region_8.9 | all-reduce | flops 4096 | bytes 32768 | tf_op jit(solution)/shard_map/pmax | solution.py:90
  114.4 0.8 copy.12
  115.3 3.5 %broadcast_multiply_fusion = f32[8,512,128]{2,1,0:T(8,128)} fusion(f32[8,512,128]{2,1,0:T(8,128)} %get-tuple-element.49, f32[8,512]{1,0:T(8,128)S(1)} %get-tuple-element.69), kind=kLoop, calls=%fused_computation.35 | loop fusion | flops 524288 | bytes 4210688 | tf_op jit(solution)/shard_map/mul | solution.py:94
  118.9 55.9 %reduce-scatter.7.cloned.1.call-done = f32[64,8]{1,0:T(8,128)} async-done(((f32[512,8]{1,0:T(8,128)}), f32[64,8]{1,0:T(8,128)}) %reduce-scatter.7.cloned.1.call-update) | async-done | bytes 2064
  174.8 0.8 copy.13
  175.6 70.5 %reduce-scatter.5.cloned.1.call-done = f32[8,64,128]{2,1,0:T(8,128)} async-done(((f32[8,512,128]{2,1,0:T(8,128)}), f32[8,64,128]{2,1,0:T(8,128)}) %reduce-scatter.5.cloned.1.call-update) | async-done | bytes 262160 | tf_op jit(solution)/shard_map/reduce_scatter | solution.py:93
  246.1 2.9 %fusion.23 = bf16[64,1024]{1,0:T(8,128)(2,1)} fusion(bf16[1024,1024]{1,0:T(8,128)(2,1)} %param.19, bf16[512,1024]{1,0:T(8,128)(2,1)S(1)} %copy-done.1, s32[]{:T(128)S(6)} %select_n.8, f32[8,64,128]{2,1,0:T(8,128)} %reduce-scatter.5.cloned.1.call-done, f32[8,64]{1,0:T(8,128)S(1)} %copy.13), kind=kOutput, calls=%fused_computation.34 | convolution fusion | flops 134545408 | bytes 2623492 | tf_op jit(solution)/shard_map/dot_general | solution.py:101
  (70 shorter events, 3.8 us)
Async XLA Ops:
  6.5 10.3 %copy-start = (bf16[1024,1024]{1,0:T(8,128)(2,1)S(1)}, bf16[1024,1024]{1,0:T(8,128)(2,1)}, u32[]{:S(2)}) copy-start(bf16[1024,1024]{1,0:T(8,128)(2,1)} %param.18) | copy-start | bytes 6291460
  6.5 10.3 %copy-start.1 = (bf16[512,1024]{1,0:T(8,128)(2,1)S(1)}, bf16[512,1024]{1,0:T(8,128)(2,1)}, u32[]{:S(2)}) copy-start(bf16[512,1024]{1,0:T(8,128)(2,1)} %param.16) | copy-start | bytes 3145732
  6.5 10.3 %copy-start.8 = (f32[1024]{0:T(1024)S(1)}, f32[1024]{0:T(1024)}, u32[]{:S(2)}) copy-start(f32[1024]{0:T(1024)} %param.17) | copy-start | bytes 12292
  6.5 168.2 %reduce-scatter.7.cloned.1.call-start = ((), (), s32[]{:S(2)}) async-start(), calls=%async_computation.3 | async-start | bytes 294912
  7.4 11.8 %collective-permute-start = (bf16[1,56,6]{1,0,2:T(2,128)(2,1)S(1)}, bf16[1,56,6]{1,0,2:T(2,128)(2,1)S(1)}, u32[]{:S(2)}, u32[]{:S(2)}) collective-permute-start(bf16[1,56,6]{1,0,2:T(2,128)(2,1)S(1)} %get-tuple-element.76), channel_id=1, source_target_pairs={{0,4},{1,5},{2,6},{3,7},{8,12},{9,13},{10,14},{11,15},{16,20},{17,... | collective-permute-start | bytes 2024 | tf_op jit(solution)/shard_map/ppermute | solution.py:18
  12.5 6.8 %collective-permute-start.1 = (bf16[1,56,6]{1,0,2:T(2,128)(2,1)S(1)}, bf16[1,56,6]{1,0,2:T(2,128)(2,1)S(1)}, u32[]{:S(2)}, u32[]{:S(2)}) collective-permute-start(bf16[1,56,6]{1,0,2:T(2,128)(2,1)S(1)} %get-tuple-element.77), channel_id=1, source_target_pairs={{4,0},{5,1},{6,2},{7,3},{12,8},{13,9},{14,10},{15,11},{20,16},{21,... | collective-permute-start | bytes 2024 | tf_op jit(solution)/shard_map/ppermute | solution.py:20
  16.9 2.4 copy-start.2
  16.9 12.4 %copy-start.3 = (bf16[54,704]{1,0:T(8,128)(2,1)S(1)}, bf16[54,704]{1,0:T(8,128)(2,1)}, u32[]{:S(2)}) copy-start(bf16[54,704]{1,0:T(8,128)(2,1)} %param.12) | copy-start | bytes 228100
  19.4 5.0 %collective-permute-start.2 = (bf16[16,1,6]{1,0,2:T(8,128)(2,1)S(1)}, bf16[16,1,6]{1,0,2:T(8,128)(2,1)S(1)}, u32[]{:S(2)}, u32[]{:S(2)}) collective-permute-start(bf16[16,1,6]{1,0,2:T(8,128)(2,1)S(1)} %get-tuple-element.75), channel_id=1, source_target_pairs={{0,1},{1,2},{2,3},{4,5},{5,6},{6,7},{8,9},{9,10},{10,11},{12,13},{... | collective-permute-start | bytes 584 | tf_op jit(solution)/shard_map/ppermute | solution.py:18
  22.8 5.7 %collective-permute-start.3 = (bf16[16,1,6]{1,0,2:T(8,128)(2,1)S(1)}, bf16[16,1,6]{1,0,2:T(8,128)(2,1)S(1)}, u32[]{:S(2)}, u32[]{:S(2)}) collective-permute-start(bf16[16,1,6]{1,0,2:T(8,128)(2,1)S(1)} %get-tuple-element.74), channel_id=1, source_target_pairs={{1,0},{2,1},{3,2},{5,4},{6,5},{7,6},{9,8},{10,9},{11,10},{13,12},{... | collective-permute-start | bytes 584 | tf_op jit(solution)/shard_map/ppermute | solution.py:20
  29.3 1.4 copy-start.6
  29.3 1.4 copy-start.9
  30.7 2.7 %copy-start.7 = (bf16[704,1024]{1,0:T(8,128)(2,1)S(1)}, bf16[704,1024]{1,0:T(8,128)(2,1)}, u32[]{:S(2)}) copy-start(bf16[704,1024]{1,0:T(8,128)(2,1)} %param.14) | copy-start | bytes 4325380
  33.4 2.7 %copy-start.4 = (f32[8,512]{1,0:T(8,128)S(1)}, f32[8,512]{1,0:T(8,128)}, u32[]{:S(2)}) copy-start(f32[8,512]{1,0:T(8,128)} %custom-call.1) | copy-start | bytes 49156
  33.4 2.7 %copy-start.5 = (f32[8,512]{1,0:T(8,128)S(1)}, f32[8,512]{1,0:T(8,128)}, u32[]{:S(2)}) copy-start(f32[8,512]{1,0:T(8,128)} %custom-call.2) | copy-start | bytes 49156
  115.3 130.8 %reduce-scatter.5.cloned.1.call-start = ((), (), s32[]{:S(2)}) async-start(), calls=%async_computation.2 | async-start | bytes 2359296 | tf_op jit(solution)/shard_map/reduce_scatter | solution.py:93
Sparse Core Ops, SparseCore 0:
  115.4 59.3 reduce-scatter.6
  178.3 67.7 reduce-scatter.4
where the time goes:
time: 257 us; the launch traced here: 256 us
  waiting for transfers between devices  131 us (51%)
  matrix products  39.1 us (15%)
  blocking collectives  36.8 us (14%)
  between operations  13.6 us (5%)
  starting transfers between devices  11.1 us (4%)
  other arithmetic  9.82 us (4%)
  local copies, waits for them, and re-layouts  8.93 us (3%)
  loops' own time  5.5 us (2%)
    reduce_scatter x1, waiting for transfers between devices, on_device(): lax.psum_scatter(local_summed * factor[..., None], ('gx', 'gy'), scatter_...  70.5 us
    unnamed x3, waiting for transfers between devices  55.9 us
    pmax x1, blocking collectives, on_device(): global_top = lax.pmax(local_top, ('gx', 'gy'))  36.8 us
    dot_general x8, matrix products, one_head(): jnp.dot(expo.astype(jnp.bfloat16), value_head, preferred_element_type=jnp...  16.9 us
    dot_general x8, matrix products, one_head(): jnp.dot(query_head, key_head.T, preferred_element_type=jnp.float32) * scale  11.1 us
    ppermute x2, starting transfers between devices, extended(): lax.ppermute(tail, axis, [(i, (i + 1) % count) for i in range(ends)])  8.49 us
    another operation x1, loops' own time, on_device(): lax.map(one_head, jnp.arange(HEADS, dtype=jnp.int32))  5.5 us
  transfers between devices with their start and end apart: 6, of which 4 were waited for; matrix products, arithmetic and copies ran while one was open for 4% of the time, Pallas kernels for 0%

commit v1 on v0

v1 whole, which is shorter than its diff:
```python
import functools
import math

import jax
import jax.numpy as jnp
from jax import lax
from jax.experimental import pallas as pl
from jax.experimental.pallas import tpu as pltpu
from jax.sharding import PartitionSpec as P

DH = 128
MESH = pl.DeviceIdType.MESH
BF = jnp.bfloat16
F32 = jnp.float32


def mm(a, b, precision=None):
    return lax.dot_general(
        a, b, (((1,), (0,)), ((), ())), precision=precision, preferred_element_type=F32
    )


def mm_nt(a, b):
    return lax.dot_general(a, b, (((1,), (1,)), ((), ())), preferred_element_type=F32)


def split(x):
    hi = x.astype(BF).astype(F32)
    return hi, x - hi


def kernel(
    dims,
    px_ref,
    conv_ref,
    gain_ref,
    lgain_ref,
    wk_ref,
    wv_ref,
    lat_ref,
    wq_ref,
    wo_ref,
    out_ref,
    tiles,
    stack,
    conv8,
    wk,
    wv,
    wq,
    lat,
    own,
    wo,
    acc,
    top,
    att_src,
    att,
    copy_sem,
    send1,
    recv1,
    send2,
    recv2,
):
    ngx, ngy, tr, tc, heads, taps, chans = dims
    g = ngx * ngy
    blocks = g // heads
    share = own.shape[0]
    rows = lat.shape[0]
    width = px_ref.shape[1]
    cells = tr * tc
    ch = px_ref.shape[0]
    pk = taps * ch
    me = lax.axis_index("gx") * ngy + lax.axis_index("gy")
    head = lax.rem(me, heads)
    block = me // heads

    col = pl.ds(pl.multiple_of(head * DH, DH), DH)
    lat_rows = pl.ds(pl.multiple_of(block * rows, rows), rows)
    own_rows = pl.ds(pl.multiple_of(me * share, share), share)
    loads = [
        pltpu.make_async_copy(px_ref, tiles.at[me], copy_sem.at[0]),
        pltpu.make_async_copy(lat_ref.at[lat_rows, :], lat, copy_sem.at[1]),
        pltpu.make_async_copy(wq_ref.at[:, col], wq, copy_sem.at[2]),
        pltpu.make_async_copy(wk_ref.at[:, col], wk, copy_sem.at[3]),
        pltpu.make_async_copy(wv_ref.at[:, col], wv, copy_sem.at[4]),
        pltpu.make_async_copy(lat_ref.at[own_rows, :], own, copy_sem.at[5]),
        pltpu.make_async_copy(wo_ref, wo, copy_sem.at[6]),
    ]
    for load in loads:
        load.start()

    def place(p):
        return {"gx": p // ngy, "gy": lax.rem(p, ngy)}

    barrier = pltpu.get_barrier_semaphore()
    for k in range(1, g):
        pl.semaphore_signal(
            barrier, inc=1, device_id=place(lax.rem(me + k, g)), device_id_type=MESH
        )
    pl.semaphore_wait(barrier, g - 1)
    sends = []
    for k in range(1, g):
        send = pltpu.make_async_remote_copy(
            src_ref=px_ref,
            dst_ref=tiles.at[me],
            send_sem=send1.at[k],
            recv_sem=recv1.at[k],
            device_id=place(lax.rem(me + k, g)),
            device_id_type=MESH,
        )
        send.start()
        sends.append(send)

    conv8[...] = jnp.zeros_like(conv8)
    for s in range(taps):
        conv8[s * ch : s * ch + chans, :] = conv_ref[s * chans : (s + 1) * chans, :].astype(F32)
    conv = conv8[...]
    centred = conv - jnp.mean(conv, axis=-1, keepdims=True)
    gained_hi, gained_lo = split(centred * gain_ref[...])
    gained = jnp.concatenate([gained_hi, gained_lo], axis=0).astype(BF)
    doubled = jnp.transpose(jnp.concatenate([centred, centred], axis=0))
    lane2 = lax.broadcasted_iota(jnp.int32, doubled.shape, 1)
    d_hi, d_lo = split(doubled)
    conv_t = jnp.where(lane2 < pk, d_hi, d_lo).astype(BF)

    loads[1].wait()
    loads[2].wait()
    rows_f = lat[...].astype(F32)
    mean = jnp.mean(rows_f, axis=-1, keepdims=True)
    rows_c = rows_f - mean
    var = jnp.mean(rows_c * rows_c, axis=-1, keepdims=True)
    lat_normed = (rows_c * lax.rsqrt(var + 1e-05) * lgain_ref[...]).astype(BF)
    query = mm(lat_normed, wq[...]).astype(BF)
    loads[3].wait()
    loads[4].wait()
    mk2 = mm(gained, wk[...])
    mv2 = mm(gained, wv[...])
    mk = mk2[:pk] + mk2[pk:]
    mv = mv2[:pk] + mv2[pk:]
    mk_hi, mk_lo = split(mk)
    mk3_hi = jnp.concatenate([mk_hi] * 3, axis=0).astype(BF)
    mk3_lo = jnp.concatenate([mk_lo] * 3, axis=0).astype(BF)
    q3 = (mm_nt(query, mk3_hi) + mm_nt(query, mk3_lo)) * (math.log2(math.e) / DH**0.5)
    q_hi, q_lo = split(q3)
    lane3 = lax.broadcasted_iota(jnp.int32, q3.shape, 1)
    q3 = jnp.where((lane3 >= pk) & (lane3 < 2 * pk), q_lo, q_hi)
    q3 = jnp.where(lane3 == chans, 1.0, q3).astype(BF)

    loads[0].wait()
    for k, send in enumerate(sends, 1):
        came = pltpu.make_async_remote_copy(
            src_ref=px_ref,
            dst_ref=tiles.at[lax.rem(me + g - k, g)],
            send_sem=send1.at[k],
            recv_sem=recv1.at[k],
            device_id=place(lax.rem(me + g - k, g)),
            device_id_type=MESH,
        )
        came.wait_recv()

    lane = lax.broadcasted_iota(jnp.int32, (ch, width), 1)
    tile_row = lane // tc
    tile_col = lane - tile_row * tc
    low_row, high_row = tile_row == 0, tile_row == tr - 1
    low_col, high_col = tile_col == 0, tile_col == tc - 1

    def roll(x, shift):
        return pltpu.roll(x, shift % width, 1)

    def build(t):
        static = isinstance(t, int)
        i = t // ngy
        j = t - i * ngy

        def get(di, dj):
            if static:
                if 0 <= i + di < ngx and 0 <= j + dj < ngy:
                    return tiles[t + di * ngy + dj]
                return None
            inside = (i + di >= 0) & (i + di < ngx) & (j + dj >= 0) & (j + dj < ngy)
            at = jnp.clip(t + di * ngy + dj, 0, g - 1)
            return tiles[at] * jnp.where(inside, 1.0, 0.0)

        def pick(mask, edge, edge_shift, inner, inner_shift):
            if inner is None and edge is None:
                return None
            a = jnp.zeros((ch, width), F32) if edge is None else roll(edge, edge_shift)
            b = jnp.zeros((ch, width), F32) if inner is None else roll(inner, inner_shift)
            return jnp.where(mask, a, b)

        def columns(di):
            mid = get(di, 0)
            left = pick(low_col, get(di, -1), 1 - tc, mid, 1)
            right = pick(high_col, get(di, 1), tc - 1, mid, -1)
            return left, mid, right

        above, here, below = columns(-1), columns(0), columns(1)
        reach = (tr - 1) * tc
        parts = [pick(low_row, a, -reach, h, tc) for a, h in zip(above, here)]
        parts += list(here)
        parts += [pick(high_row, b, reach, h, -tc) for b, h in zip(below, here)]
        patches = jnp.concatenate(parts, axis=0)
        twice = jnp.concatenate([patches, patches], axis=0).astype(BF)
        feats = mm(conv_t, twice)
        variance = jnp.sum(feats * feats, axis=0, keepdims=True) * (1.0 / conv_t.shape[0])
        scaled = patches * lax.rsqrt(variance + 1e-05)
        hi, lo = split(scaled)
        full = jnp.concatenate([hi, hi, lo], axis=0)
        row3 = lax.broadcasted_iota(jnp.int32, full.shape, 0)
        cell3 = lax.broadcasted_iota(jnp.int32, full.shape, 1)
        full = jnp.where((row3 == chans) & (cell3 >= cells), -1e30, full)
        full = jnp.where(row3 == chans + 1, 1.0, full)
        stack[t] = full.astype(BF)

    def attend(t, first):
        block_px = stack[t]
        scores = mm(q3, block_px)
        high = jnp.max(scores, axis=-1, keepdims=True)
        if not first:
            high = jnp.maximum(high, top[...])
        expo = jnp.exp2(scores - high).astype(BF)
        part = mm_nt(expo, block_px)
        if first:
            acc[...] = part
        else:
            acc[...] = acc[...] * jnp.exp2(top[...] - high) + part
        top[...] = high

    if g <= 8:
        for t in range(g):
            build(t)
        for t in range(g):
            attend(t, t == 0)
    else:
        pl.loop(0, g)(build)
        attend(0, True)
        pl.loop(1, g)(lambda t: attend(t, False))

    summed = acc[...]
    lane_s = lax.broadcasted_iota(jnp.int32, summed.shape, 1)
    total = jnp.sum(jnp.where(lane_s == chans + 1, summed, 0.0), axis=-1, keepdims=True)
    mv3 = jnp.concatenate([mv, jnp.zeros_like(mv), mv], axis=0)
    attended = mm(summed / total, mv3, precision=lax.Precision.HIGHEST)
    att_src[...] = attended.astype(BF).reshape(heads, share, DH)

    mine = pltpu.make_async_copy(att_src.at[head], att.at[head], copy_sem.at[7])
    mine.start()
    sends2 = []
    for k in range(1, heads):
        to = lax.rem(head + k, heads)
        send = pltpu.make_async_remote_copy(
            src_ref=att_src.at[to],
            dst_ref=att.at[head],
            send_sem=send2.at[k],
            recv_sem=recv2.at[k],
            device_id=place(block * heads + to),
            device_id_type=MESH,
        )
        send.start()
        sends2.append(send)
    for send in sends:
        send.wait_send()
    loads[5].wait()
    loads[6].wait()
    mine.wait()
    for k in range(1, heads):
        source = lax.rem(head + heads - k, heads)
        came = pltpu.make_async_remote_copy(
            src_ref=att_src.at[source],
            dst_ref=att.at[source],
            send_sem=send2.at[k],
            recv_sem=recv2.at[k],
            device_id=place(block * heads + source),
            device_id_type=MESH,
        )
        came.wait_recv()
    gathered = jnp.concatenate([att[h] for h in range(heads)], axis=1)
    out_ref[...] = (own[...].astype(F32) + mm(gathered, wo[...])).astype(BF)
    for send in sends2:
        send.wait_send()


def on_device(
    pixels,
    conv_weight,
    input_gain,
    key_weight,
    value_weight,
    latents,
    latent_gain,
    query_weight,
    out_weight,
):
    tr, tc, chans = pixels.shape
    ngx, ngy = lax.axis_size("gx"), lax.axis_size("gy")
    g = ngx * ngy
    lat_count, width_d = latents.shape
    heads = width_d // DH
    share = lat_count // g
    rows = share * heads
    feat = conv_weight.shape[1]
    taps = conv_weight.shape[0] // chans
    width = -(-tr * tc // 128) * 128
    ch = -(-(chans + 2) // 8) * 8
    flat = jnp.transpose(pixels, (2, 0, 1)).reshape(chans, tr * tc).astype(F32)
    flat = jnp.pad(flat, ((0, ch - chans), (0, width - tr * tc)))
    pk = taps * ch
    vmem = pl.BlockSpec(memory_space=pltpu.VMEM)
    hbm = pl.BlockSpec(memory_space=pl.ANY)
    return pl.pallas_call(
        functools.partial(kernel, (ngx, ngy, tr, tc, heads, taps, chans)),
        out_shape=jax.ShapeDtypeStruct((share, width_d), BF),
        in_specs=[vmem] * 4 + [hbm] * 5,
        out_specs=vmem,
        scratch_shapes=[
            pltpu.VMEM((g, ch, width), F32),
            pltpu.VMEM((g, 3 * pk, width), BF),
            pltpu.VMEM((pk, feat), F32),
            pltpu.VMEM((feat, DH), BF),
            pltpu.VMEM((feat, DH), BF),
            pltpu.VMEM((width_d, DH), BF),
            pltpu.VMEM((rows, width_d), BF),
            pltpu.VMEM((share, width_d), BF),
            pltpu.VMEM((width_d, width_d), BF),
            pltpu.VMEM((rows, 3 * pk), F32),
            pltpu.VMEM((rows, 1), F32),
            pltpu.VMEM((heads, share, DH), BF),
            pltpu.VMEM((heads, share, DH), BF),
            pltpu.SemaphoreType.DMA((8,)),
            pltpu.SemaphoreType.DMA((g,)),
            pltpu.SemaphoreType.DMA((g,)),
            pltpu.SemaphoreType.DMA((heads,)),
            pltpu.SemaphoreType.DMA((heads,)),
        ],
        compiler_params=pltpu.CompilerParams(
            collective_id=0, has_side_effects=True, vmem_limit_bytes=56 * 1024 * 1024
        ),
    )(
        flat,
        conv_weight,
        input_gain.reshape(1, -1),
        latent_gain.reshape(1, -1),
        key_weight,
        value_weight,
        latents,
        query_weight,
        out_weight,
    )


def solution(mesh):
    return jax.shard_map(
        on_device,
        mesh=mesh,
        in_specs=(P(("ba", "gx"), "gy", None), P(), P(), P(), P(), P(), P(), P(), P()),
        out_specs=P(("ba", "gx", "gy"), None),
        check_vma=False,
    )
```

time: 257 us -> 34 us (0.13)
  waiting for transfers between devices: 131 us -> 0 us
  matrix products: 39.1 us -> 0 us
  blocking collectives: 36.8 us -> 0 us
  Pallas kernels: 0 us -> 29.4 us
  between operations: 13.6 us -> 0.02 us
  starting transfers between devices: 11.1 us -> 0 us
  other arithmetic: 9.82 us -> 0.62 us
  loops' own time: 5.5 us -> 0 us
  local copies, waits for them, and re-layouts: 8.93 us -> 3.68 us
    reduce_scatter x1 -> x0, waiting for transfers between devices: 70.5 us -> none  [on_device(): lax.psum_scatter(local_summed * factor[..., None], ('gx', 'gy'), scatter_...]
    unnamed x3 -> x0, waiting for transfers between devices: 55.9 us -> none
    dot_general x21 -> x0, matrix products: 39.1 us -> none  [the longest x8 16.9 us: one_head(): jnp.dot(expo.astype(jnp.bfloat16), value_head, preferred_element_type=jnp...]
    pmax x1 -> x0, blocking collectives: 36.8 us -> none  [on_device(): global_top = lax.pmax(local_top, ('gx', 'gy'))]
    pallas_call x0 -> x1, Pallas kernels: none -> 29.4 us  [on_device(): pl.pallas_call(functools.partial(kernel, (ngx, ngy, tr, tc, heads, taps,...]
    ppermute x4 -> x0, starting transfers between devices: 11.1 us -> none  [the longest x2 8.49 us: extended(): lax.ppermute(tail, axis, [(i, (i + 1) % count) for i in range(ends)])]
    reduce_sum x11 -> x0, other arithmetic: 6.1 us -> none  [the longest x8 2.47 us: one_head(): total = jnp.sum(expo, axis=-1)]
    another operation x1 -> x0, loops' own time: 5.5 us -> none  [on_device(): lax.map(one_head, jnp.arange(HEADS, dtype=jnp.int32))]
  transfers between devices with their start and end apart: 6 -> 0, of which waited for: 4 -> 0; matrix products, arithmetic and copies ran while one was open for 4% -> 0% of each run, Pallas kernels for 0% -> 0%
where the time goes in v1:
time: 34 us; the launch traced here: 33.8 us
  Pallas kernels  29.4 us (86%)
  local copies, waits for them, and re-layouts  3.68 us (11%)
  other arithmetic  0.62 us (2%)
    pallas_call x1, Pallas kernels, on_device(): pl.pallas_call(functools.partial(kernel, (ngx, ngy, tr, tc, heads, taps,...  29.4 us
    unnamed x1, local copies, waits for them, and re-layouts  1.57 us
    reshape x1, local copies, waits for them, and re-layouts, on_device(): input_gain.reshape(1, -1)  1.27 us
    convert_element_type x1, local copies, waits for them, and re-layouts, on_device(): flat = jnp.transpose(pixels, (2, 0, 1)).reshape(chans, tr * tc).astype(F32)  0.83 us

profile of v1, /device:TPU:0, one launch (start us, length us, event | category | flops | bytes accessed | tf_op | source)
XLA Modules:
  0.0 33.8 jit_solution(5361821212297810416)
XLA Ops:
  0.0 1.3 %reshape.9.gain_ref = f32[1,704]{1,0:T(1,128)} reshape(f32[704]{0:T(1024)} %param.11) | data formatting | bytes 5632 | tf_op jit(solution)/shard_map/reshape | solution.py:340
  1.3 0.8 %convert_element_type.10 = bf16[6,784]{1,0:T(8,128)(2,1)S(1)} reshape(bf16[6,14,56]{2,1,0:T(8,128)(2,1)} %bitcast.2) | data formatting | bytes 18816 | tf_op jit(solution)/shard_map/convert_element_type | solution.py:304
  2.1 0.6 %pad_convert_fusion.px_ref = f32[8,896]{1,0:T(8,128)} fusion(bf16[6,784]{1,0:T(8,128)(2,1)S(1)} %convert_element_type.10), kind=kLoop, calls=%fused_computation | loop fusion | flops 7168 | bytes 38080 | tf_op jit(solution)/shard_map/jit(_pad)/pad | solution.py:305
  2.7 29.4 %shard_map.91 = bf16[64,1024]{1,0:T(8,128)(2,1)} custom-call(f32[8,896]{1,0:T(8,128)} %pad_convert_fusion.px_ref, bf16[54,704]{1,0:T(8,128)(2,1)} %conv_ref.1, f32[1,704]{1,0:T(1,128)} %reshape.9.gain_ref, f32[1,1024]{1,0:T(1,128)} %bitcast.3, bf16[704,1024]{1,0:T(8,128)(2,1)} %wk_ref.1, bf16[704,1024]{1,0:T(8,128)(2,1)} %wv_ref.1, ...), custom_call_target="tpu_custom_call" | custom-call | tf_op jit(solution)/shard_map/pallas_call | solution.py:309
  32.2 1.6 %copy.11 = bf16[64,1024]{1,0:T(8,128)(2,1)} copy(bf16[64,1024]{1,0:T(8,128)(2,1)} %shard_map.91) | data formatting | bytes 262144

commit v2 on v1

--- a/solution.py
+++ b/solution.py
@@ -31,16 +31,24 @@
 
 def kernel(
     dims,
-    px_ref,
-    conv_ref,
-    gain_ref,
-    lgain_ref,
+    px_hbm,
+    conv_hbm,
+    gain_hbm,
+    lgain_hbm,
     wk_ref,
     wv_ref,
     lat_ref,
     wq_ref,
     wo_ref,
     out_ref,
+    px_raw,
+    px_wide,
+    px_ref,
+    conv_ref,
+    gain_ref,
+    lgain_ref,
+    code_ref,
+    patch_ref,
     tiles,
     stack,
     conv8,
@@ -66,6 +74,7 @@
     share = own.shape[0]
     rows = lat.shape[0]
     width = px_ref.shape[1]
+    compact = g <= 8
     cells = tr * tc
     ch = px_ref.shape[0]
     pk = taps * ch
@@ -76,8 +85,25 @@
     col = pl.ds(pl.multiple_of(head * DH, DH), DH)
     lat_rows = pl.ds(pl.multiple_of(block * rows, rows), rows)
     own_rows = pl.ds(pl.multiple_of(me * share, share), share)
+    def place(p):
+        return {"gx": p // ngy, "gy": lax.rem(p, ngy)}
+
+    barrier = pltpu.get_barrier_semaphore()
+    for k in range(1, g):
+        pl.semaphore_signal(
+            barrier, inc=1, device_id=place(lax.rem(me + k, g)), device_id_type=MESH
+        )
+    early = [
+        pltpu.make_async_copy(px_hbm, px_raw, copy_sem.at[8]),
+        pltpu.make_async_copy(conv_hbm, conv_ref, copy_sem.at[9]),
+        pltpu.make_async_copy(gain_hbm, gain_ref, copy_sem.at[10]),
+        pltpu.make_async_copy(lgain_hbm, lgain_ref, copy_sem.at[11]),
+    ]
+    for load in early:
+        load.start()
+    own_tile = pltpu.make_async_copy(px_ref, tiles.at[me], copy_sem.at[0])
     loads = [
-        pltpu.make_async_copy(px_ref, tiles.at[me], copy_sem.at[0]),
+        own_tile,
         pltpu.make_async_copy(lat_ref.at[lat_rows, :], lat, copy_sem.at[1]),
         pltpu.make_async_copy(wq_ref.at[:, col], wq, copy_sem.at[2]),
         pltpu.make_async_copy(wk_ref.at[:, col], wk, copy_sem.at[3]),
@@ -85,17 +111,31 @@
         pltpu.make_async_copy(lat_ref.at[own_rows, :], own, copy_sem.at[5]),
         pltpu.make_async_copy(wo_ref, wo, copy_sem.at[6]),
     ]
-    for load in loads:
+    for load in loads[1:]:
         load.start()
 
-    def place(p):
-        return {"gx": p // ngy, "gy": lax.rem(p, ngy)}
-
-    barrier = pltpu.get_barrier_semaphore()
-    for k in range(1, g):
-        pl.semaphore_signal(
-            barrier, inc=1, device_id=place(lax.rem(me + k, g)), device_id_type=MESH
-        )
+    px_wide[...] = jnp.zeros_like(px_wide)
+    if compact:
+        spot = lax.broadcasted_iota(jnp.int32, (ch, g * cells), 1)
+        tile = spot // cells
+        inner = spot - tile * cells
+        r = inner // tc
+        c = inner - r * tc
+        ti = tile // ngy
+        tj = tile - ti * ngy
+        code = jnp.zeros_like(spot)
+        tests = (
+            c == 0, c == tc - 1, r == 0, r == tr - 1,
+            tj == 0, tj == ngy - 1, ti == 0, ti == ngx - 1,
+        )
+        for bit, test in enumerate(tests):
+            code = code + jnp.where(test, 1 << bit, 0)
+        code_ref[...] = code
+    early[0].wait()
+    raw = px_raw[...].astype(F32)
+    px_wide[0:chans, 0:cells] = jnp.concatenate([raw[:, r, :] for r in range(tr)], axis=1)
+    px_ref[...] = px_wide[...].astype(BF)
+    own_tile.start()
     pl.semaphore_wait(barrier, g - 1)
     sends = []
     for k in range(1, g):
@@ -110,12 +150,14 @@
         send.start()
         sends.append(send)
 
+    for load in early[1:]:
+        load.wait()
     conv8[...] = jnp.zeros_like(conv8)
     for s in range(taps):
         conv8[s * ch : s * ch + chans, :] = conv_ref[s * chans : (s + 1) * chans, :].astype(F32)
     conv = conv8[...]
     centred = conv - jnp.mean(conv, axis=-1, keepdims=True)
-    gained_hi, gained_lo = split(centred * gain_ref[...])
+    gained_hi, gained_lo = split(centred * gain_ref[...].reshape(1, -1))
     gained = jnp.concatenate([gained_hi, gained_lo], axis=0).astype(BF)
     doubled = jnp.transpose(jnp.concatenate([centred, centred], axis=0))
     lane2 = lax.broadcasted_iota(jnp.int32, doubled.shape, 1)
@@ -128,7 +170,7 @@
     mean = jnp.mean(rows_f, axis=-1, keepdims=True)
     rows_c = rows_f - mean
     var = jnp.mean(rows_c * rows_c, axis=-1, keepdims=True)
-    lat_normed = (rows_c * lax.rsqrt(var + 1e-05) * lgain_ref[...]).astype(BF)
+    lat_normed = (rows_c * lax.rsqrt(var + 1e-05) * lgain_ref[...].reshape(1, -1)).astype(BF)
     query = mm(lat_normed, wq[...]).astype(BF)
     loads[3].wait()
     loads[4].wait()
@@ -174,11 +216,11 @@
         def get(di, dj):
             if static:
                 if 0 <= i + di < ngx and 0 <= j + dj < ngy:
-                    return tiles[t + di * ngy + dj]
+                    return tiles[t + di * ngy + dj].astype(F32)
                 return None
             inside = (i + di >= 0) & (i + di < ngx) & (j + dj >= 0) & (j + dj < ngy)
             at = jnp.clip(t + di * ngy + dj, 0, g - 1)
-            return tiles[at] * jnp.where(inside, 1.0, 0.0)
+            return tiles[at].astype(F32) * jnp.where(inside, 1.0, 0.0)
 
         def pick(mask, edge, edge_shift, inner, inner_shift):
             if inner is None and edge is None:
@@ -199,6 +241,13 @@
         parts += list(here)
         parts += [pick(high_row, b, reach, h, -tc) for b, h in zip(below, here)]
         patches = jnp.concatenate(parts, axis=0)
+        full = finish(patches)
+        row3 = lax.broadcasted_iota(jnp.int32, full.shape, 0)
+        cell3 = lax.broadcasted_iota(jnp.int32, full.shape, 1)
+        full = jnp.where((row3 == chans) & (cell3 >= cells), -1e30, full)
+        stack[t] = full.astype(BF)
+
+    def finish(patches):
         twice = jnp.concatenate([patches, patches], axis=0).astype(BF)
         feats = mm(conv_t, twice)
         variance = jnp.sum(feats * feats, axis=0, keepdims=True) * (1.0 / conv_t.shape[0])
@@ -206,13 +255,9 @@
         hi, lo = split(scaled)
         full = jnp.concatenate([hi, hi, lo], axis=0)
         row3 = lax.broadcasted_iota(jnp.int32, full.shape, 0)
-        cell3 = lax.broadcasted_iota(jnp.int32, full.shape, 1)
-        full = jnp.where((row3 == chans) & (cell3 >= cells), -1e30, full)
-        full = jnp.where(row3 == chans + 1, 1.0, full)
-        stack[t] = full.astype(BF)
-
-    def attend(t, first):
-        block_px = stack[t]
+        return jnp.where(row3 == chans + 1, 1.0, full)
+
+    def attend(block_px, first):
         scores = mm(q3, block_px)
         high = jnp.max(scores, axis=-1, keepdims=True)
         if not first:
@@ -225,21 +270,62 @@
             acc[...] = acc[...] * jnp.exp2(top[...] - high) + part
         top[...] = high
 
-    if g <= 8:
-        for t in range(g):
-            build(t)
-        for t in range(g):
-            attend(t, t == 0)
+    def build_frame():
+        frame = jnp.concatenate([tiles[t].astype(F32)[:, :cells] for t in range(g)], axis=1)
+        span = g * cells
+        code = code_ref[...]
+        low_c, high_c, low_r, high_r, left_t, right_t, top_t, bottom_t = (
+            (code & (1 << bit)) != 0 for bit in range(8)
+        )
+
+        def shifted(x, edge, outside, far, near):
+            far_x = jnp.where(outside, 0.0, pltpu.roll(x, far % span, 1))
+            return jnp.where(edge, far_x, pltpu.roll(x, near % span, 1))
+
+        side = cells - (tc - 1)
+        over = ngy * cells - (tr - 1) * tc
+        here = (
+            shifted(frame, low_c, left_t, side, 1),
+            frame,
+            shifted(frame, high_c, right_t, -side, -1),
+        )
+        parts = [shifted(x, low_r, top_t, over, tc) for x in here]
+        parts += list(here)
+        parts += [shifted(x, high_r, bottom_t, -over, -tc) for x in here]
+        for s, part in enumerate(parts):
+            patch_ref[s * ch : (s + 1) * ch, :] = part
+
+    if compact:
+        build_frame()
+        step = 2 * width
+        starts = list(range(0, g * cells, step))
+        for start in starts:
+            stop = min(start + step, g * cells)
+            stack[:, start:stop] = finish(patch_ref[:, start:stop]).astype(BF)
+        for start in starts:
+            stop = min(start + step, g * cells)
+            attend(stack[:, start:stop], start == 0)
     else:
         pl.loop(0, g)(build)
-        attend(0, True)
-        pl.loop(1, g)(lambda t: attend(t, False))
+        attend(stack[0], True)
+        pl.loop(1, g)(lambda t: attend(stack[t], False))
 
     summed = acc[...]
     lane_s = lax.broadcasted_iota(jnp.int32, summed.shape, 1)
     total = jnp.sum(jnp.where(lane_s == chans + 1, summed, 0.0), axis=-1, keepdims=True)
-    mv3 = jnp.concatenate([mv, jnp.zeros_like(mv), mv], axis=0)
-    attended = mm(summed / total, mv3, precision=lax.Precision.HIGHEST)
+    mv_hi, mv_lo = split(mv)
+    zero = jnp.zeros_like(mv_lo)
+    mv3 = jnp.concatenate(
+        [
+            jnp.concatenate([mv_hi] * 3, axis=0),
+            jnp.concatenate([mv_lo, zero, zero], axis=0),
+        ],
+        axis=1,
+    ).astype(BF)
+    s_hi, s_lo = split(summed)
+    summed3 = jnp.where((lane_s >= pk) & (lane_s < 2 * pk), s_lo, s_hi).astype(BF)
+    both = mm(summed3, mv3)
+    attended = (both[:, :DH] + both[:, DH:]) / total
     att_src[...] = attended.astype(BF).reshape(heads, share, DH)
 
     mine = pltpu.make_async_copy(att_src.at[head], att.at[head], copy_sem.at[7])
@@ -301,19 +387,27 @@
     taps = conv_weight.shape[0] // chans
     width = -(-tr * tc // 128) * 128
     ch = -(-(chans + 2) // 8) * 8
-    flat = jnp.transpose(pixels, (2, 0, 1)).reshape(chans, tr * tc).astype(F32)
-    flat = jnp.pad(flat, ((0, ch - chans), (0, width - tr * tc)))
+    planes = jnp.transpose(pixels, (2, 0, 1))
     pk = taps * ch
+    compact = g <= 8
     vmem = pl.BlockSpec(memory_space=pltpu.VMEM)
     hbm = pl.BlockSpec(memory_space=pl.ANY)
     return pl.pallas_call(
         functools.partial(kernel, (ngx, ngy, tr, tc, heads, taps, chans)),
         out_shape=jax.ShapeDtypeStruct((share, width_d), BF),
-        in_specs=[vmem] * 4 + [hbm] * 5,
+        in_specs=[hbm] * 9,
         out_specs=vmem,
         scratch_shapes=[
-            pltpu.VMEM((g, ch, width), F32),
-            pltpu.VMEM((g, 3 * pk, width), BF),
+            pltpu.VMEM((chans, tr, tc), BF),
+            pltpu.VMEM((ch, width), F32),
+            pltpu.VMEM((ch, width), BF),
+            pltpu.VMEM(conv_weight.shape, BF),
+            pltpu.VMEM((feat,), F32),
+            pltpu.VMEM((width_d,), F32),
+            pltpu.VMEM((ch, g * tr * tc if compact else 128), jnp.int32),
+            pltpu.VMEM((pk, g * tr * tc if compact else 128), F32),
+            pltpu.VMEM((g, ch, width), BF),
+            pltpu.VMEM((3 * pk, g * tr * tc) if compact else (g, 3 * pk, width), BF),
             pltpu.VMEM((pk, feat), F32),
             pltpu.VMEM((feat, DH), BF),
             pltpu.VMEM((feat, DH), BF),
@@ -325,7 +419,7 @@
             pltpu.VMEM((rows, 1), F32),
             pltpu.VMEM((heads, share, DH), BF),
             pltpu.VMEM((heads, share, DH), BF),
-            pltpu.SemaphoreType.DMA((8,)),
+            pltpu.SemaphoreType.DMA((12,)),
             pltpu.SemaphoreType.DMA((g,)),
             pltpu.SemaphoreType.DMA((g,)),
             pltpu.SemaphoreType.DMA((heads,)),
@@ -335,10 +429,10 @@
             collective_id=0, has_side_effects=True, vmem_limit_bytes=56 * 1024 * 1024
         ),
     )(
-        flat,
+        planes,
         conv_weight,
-        input_gain.reshape(1, -1),
-        latent_gain.reshape(1, -1),
+        input_gain,
+        latent_gain,
         key_weight,
         value_weight,
         latents,

time: 34 us -> 25.4 us (0.75)
  Pallas kernels: 29.4 us -> 23.7 us
  local copies, waits for them, and re-layouts: 3.68 us -> 1.57 us
  other arithmetic: 0.62 us -> 0 us
    pallas_call x1, Pallas kernels: 29.4 us -> 23.7 us  [on_device(): pl.pallas_call(functools.partial(kernel, (ngx, ngy, tr, tc, heads, taps,...]
    reshape x1 -> x0, local copies, waits for them, and re-layouts: 1.27 us -> none  [on_device(): input_gain.reshape(1, -1)]
    convert_element_type x1 -> x0, local copies, waits for them, and re-layouts: 0.83 us -> none  [on_device(): flat = jnp.transpose(pixels, (2, 0, 1)).reshape(chans, tr * tc).astype(F32)]
    pad x1 -> x0, other arithmetic: 0.62 us -> none  [on_device(): flat = jnp.pad(flat, ((0, ch - chans), (0, width - tr * tc)))]
where the time goes in v2:
time: 25.4 us; the launch traced here: 25.2 us
  Pallas kernels  23.7 us (93%)
  local copies, waits for them, and re-layouts  1.57 us (6%)
    pallas_call x1, Pallas kernels, on_device(): pl.pallas_call(functools.partial(kernel, (ngx, ngy, tr, tc, heads, taps,...  23.7 us
    unnamed x1, local copies, waits for them, and re-layouts  1.57 us

profile of v2, /device:TPU:0, one launch (start us, length us, event | category | flops | bytes accessed | tf_op | source)
XLA Modules:
  0.0 25.2 jit_solution(256841055179720883)
XLA Ops:
  0.0 23.7 %shard_map.91 = bf16[64,1024]{1,0:T(8,128)(2,1)} custom-call(bf16[6,14,56]{2,1,0:T(8,128)(2,1)} %bitcast.1, bf16[54,704]{1,0:T(8,128)(2,1)} %conv_hbm.1, f32[704]{0:T(1024)} %gain_hbm.1, f32[1024]{0:T(1024)} %lgain_hbm.1, bf16[704,1024]{1,0:T(8,128)(2,1)} %wk_ref.1, bf16[704,1024]{1,0:T(8,128)(2,1)} %wv_ref.1, bf16[512,1024]{1,0:T(8,128)(2,1)} %lat_ref.1, ...), custom_call_target="tpu_custom_call" | custom-call | tf_op jit(solution)/shard_map/pallas_call | solution.py:395
  23.7 1.6 %copy.11 = bf16[64,1024]{1,0:T(8,128)(2,1)} copy(bf16[64,1024]{1,0:T(8,128)(2,1)} %shard_map.91) | data formatting | bytes 262144

commit v3 on v2

--- a/solution.py
+++ b/solution.py
@@ -60,6 +60,7 @@
     wo,
     acc,
     top,
+    q_ref,
     att_src,
     att,
     copy_sem,
@@ -186,6 +187,7 @@
     lane3 = lax.broadcasted_iota(jnp.int32, q3.shape, 1)
     q3 = jnp.where((lane3 >= pk) & (lane3 < 2 * pk), q_lo, q_hi)
     q3 = jnp.where(lane3 == chans, 1.0, q3).astype(BF)
+    q_ref[...] = q3
 
     loads[0].wait()
     for k, send in enumerate(sends, 1):
@@ -302,59 +304,89 @@
         for start in starts:
             stop = min(start + step, g * cells)
             stack[:, start:stop] = finish(patch_ref[:, start:stop]).astype(BF)
-        for start in starts:
-            stop = min(start + step, g * cells)
-            attend(stack[:, start:stop], start == 0)
     else:
         pl.loop(0, g)(build)
         attend(stack[0], True)
         pl.loop(1, g)(lambda t: attend(stack[t], False))
 
-    summed = acc[...]
-    lane_s = lax.broadcasted_iota(jnp.int32, summed.shape, 1)
-    total = jnp.sum(jnp.where(lane_s == chans + 1, summed, 0.0), axis=-1, keepdims=True)
-    mv_hi, mv_lo = split(mv)
-    zero = jnp.zeros_like(mv_lo)
-    mv3 = jnp.concatenate(
-        [
-            jnp.concatenate([mv_hi] * 3, axis=0),
-            jnp.concatenate([mv_lo, zero, zero], axis=0),
-        ],
-        axis=1,
-    ).astype(BF)
-    s_hi, s_lo = split(summed)
-    summed3 = jnp.where((lane_s >= pk) & (lane_s < 2 * pk), s_lo, s_hi).astype(BF)
-    both = mm(summed3, mv3)
-    attended = (both[:, :DH] + both[:, DH:]) / total
-    att_src[...] = attended.astype(BF).reshape(heads, share, DH)
-
-    mine = pltpu.make_async_copy(att_src.at[head], att.at[head], copy_sem.at[7])
-    mine.start()
+    def finalize(summed):
+        lane_s = lax.broadcasted_iota(jnp.int32, summed.shape, 1)
+        total = jnp.sum(jnp.where(lane_s == chans + 1, summed, 0.0), axis=-1, keepdims=True)
+        mv_hi, mv_lo = split(mv)
+        zero = jnp.zeros_like(mv_lo)
+        mv3 = jnp.concatenate(
+            [
+                jnp.concatenate([mv_hi] * 3, axis=0),
+                jnp.concatenate([mv_lo, zero, zero], axis=0),
+            ],
+            axis=1,
+        ).astype(BF)
+        s_hi, s_lo = split(summed)
+        summed3 = jnp.where((lane_s >= pk) & (lane_s < 2 * pk), s_lo, s_hi).astype(BF)
+        both = mm(summed3, mv3)
+        attended = (both[:, :DH] + both[:, DH:]) / total
+        return attended.astype(BF)
+
+    half = heads // 2
+    far = 1 - head // half
+    spot_h = lax.rem(head, half)
     sends2 = []
-    for k in range(1, heads):
-        to = lax.rem(head + k, heads)
-        send = pltpu.make_async_remote_copy(
-            src_ref=att_src.at[to],
-            dst_ref=att.at[head],
-            send_sem=send2.at[k],
-            recv_sem=recv2.at[k],
-            device_id=place(block * heads + to),
-            device_id_type=MESH,
-        )
-        send.start()
-        sends2.append(send)
+    routes = []
+
+    def exchange(part, count_from, slot):
+        for m in range(count_from, half):
+            to = part * half + lax.rem(spot_h + m, half)
+            source = part * half + lax.rem(spot_h + half - m, half)
+            send = pltpu.make_async_remote_copy(
+                src_ref=att_src.at[to],
+                dst_ref=att.at[head],
+                send_sem=send2.at[slot + m],
+                recv_sem=recv2.at[slot + m],
+                device_id=place(block * heads + to),
+                device_id_type=MESH,
+            )
+            send.start()
+            sends2.append(send)
+            routes.append((source, slot + m))
+
+    if compact:
+        piece = rows // 2
+        for part in (far, 1 - far):
+            query_part = q_ref[pl.ds(pl.multiple_of(part * piece, piece), piece), :]
+            summed, peak = None, None
+            for start in starts:
+                block_px = stack[:, start : min(start + step, g * cells)]
+                scores = mm(query_part, block_px)
+                high = jnp.max(scores, axis=-1, keepdims=True)
+                if summed is not None:
+                    high = jnp.maximum(high, peak)
+                expo = jnp.exp2(scores - high).astype(BF)
+                added = mm_nt(expo, block_px)
+                summed = added if summed is None else summed * jnp.exp2(peak - high) + added
+                peak = high
+            att_src[pl.ds(part * half, half)] = finalize(summed).reshape(half, share, DH)
+            if part is far:
+                exchange(far, 0, 0)
+        mine = pltpu.make_async_copy(att_src.at[head], att.at[head], copy_sem.at[7])
+        mine.start()
+        exchange(1 - far, 1, half)
+    else:
+        att_src[...] = finalize(acc[...]).reshape(heads, share, DH)
+        exchange(far, 0, 0)
+        mine = pltpu.make_async_copy(att_src.at[head], att.at[head], copy_sem.at[7])
+        mine.start()
+        exchange(1 - far, 1, half)
     for send in sends:
         send.wait_send()
     loads[5].wait()
     loads[6].wait()
     mine.wait()
-    for k in range(1, heads):
-        source = lax.rem(head + heads - k, heads)
+    for source, slot in routes:
         came = pltpu.make_async_remote_copy(
             src_ref=att_src.at[source],
             dst_ref=att.at[source],
-            send_sem=send2.at[k],
-            recv_sem=recv2.at[k],
+            send_sem=send2.at[slot],
+            recv_sem=recv2.at[slot],
             device_id=place(block * heads + source),
             device_id_type=MESH,
         )
@@ -417,6 +449,7 @@
             pltpu.VMEM((width_d, width_d), BF),
             pltpu.VMEM((rows, 3 * pk), F32),
             pltpu.VMEM((rows, 1), F32),
+            pltpu.VMEM((rows, 3 * pk), BF),
             pltpu.VMEM((heads, share, DH), BF),
             pltpu.VMEM((heads, share, DH), BF),
             pltpu.SemaphoreType.DMA((12,)),

time: 25.4 us -> 24.6 us (0.969)
  Pallas kernels: 23.7 us -> 22.9 us
    pallas_call x1, Pallas kernels: 23.7 us -> 22.9 us  [on_device(): pl.pallas_call(functools.partial(kernel, (ngx, ngy, tr, tc, heads, taps,...]
where the time goes in v3:
time: 24.6 us; the launch traced here: 24.5 us
  Pallas kernels  22.9 us (93%)
  local copies, waits for them, and re-layouts  1.57 us (6%)
    pallas_call x1, Pallas kernels, on_device(): pl.pallas_call(functools.partial(kernel, (ngx, ngy, tr, tc, heads, taps,...  22.9 us
    unnamed x1, local copies, waits for them, and re-layouts  1.57 us

profile of v3, /device:TPU:0, one launch (start us, length us, event | category | flops | bytes accessed | tf_op | source)
XLA Modules:
  0.0 24.5 jit_solution(11526168644761618848)
XLA Ops:
  0.0 22.9 %shard_map.91 = bf16[64,1024]{1,0:T(8,128)(2,1)} custom-call(bf16[6,14,56]{2,1,0:T(8,128)(2,1)} %bitcast.1, bf16[54,704]{1,0:T(8,128)(2,1)} %conv_hbm.1, f32[704]{0:T(1024)} %gain_hbm.1, f32[1024]{0:T(1024)} %lgain_hbm.1, bf16[704,1024]{1,0:T(8,128)(2,1)} %wk_ref.1, bf16[704,1024]{1,0:T(8,128)(2,1)} %wv_ref.1, bf16[512,1024]{1,0:T(8,128)(2,1)} %lat_ref.1, ...), custom_call_target="tpu_custom_call" | custom-call | tf_op jit(solution)/shard_map/pallas_call | solution.py:427
  22.9 1.6 %copy.11 = bf16[64,1024]{1,0:T(8,128)(2,1)} copy(bf16[64,1024]{1,0:T(8,128)(2,1)} %shard_map.91) | data formatting | bytes 262144
